TPU v7x, 32 devices: a whole 2x2x4 slice. The times are simulated.
32 devices in a mesh: pts: 8 (over z, y), hrs: 4 (over x, core).
Axes of the slice: x: 2, y: 2, z: 4, core: 2. Of those that a mesh axis runs over, the one named last changes fastest.
Arguments:
- fields: float32 [512, 65536], P(('pts', 'hrs')), may hold values from -2000 to 2000, as said below
- probes: float32 [256, 512], replicated, may hold values from -0.25 to 0.25
Outputs:
- basis_rows: float32 [256, 65536], P(None, ('pts', 'hrs'))
- coeffs: float32 [256, 512], replicated
Inputs may be any that keep to these rules, and one draw needn't show every extreme that they name: `fields`: every hour and every grid point carries its own scale, and the values are real-valued and never all zero.
All inputs are finite; a program needn't handle non-finite values.
Results may differ from a plain program's by a relative error of at most 0.00017.
Values sent between devices are 32-bit elements; how exact they have to be, the bound alone decides.
A program may use at most 64 MiB of HBM per device.

v0:
```python
import jax
import jax.numpy as jnp
from jax import lax
from jax.sharding import PartitionSpec as P

highest = lax.Precision.HIGHEST


def contract_last(left, right):
    return lax.dot_general(
        left, right, (((1,), (1,)), ((), ())), precision=highest, preferred_element_type=jnp.float32
    )


def on_device(fields, probes):
    n_pts = lax.axis_size("pts")
    n_hrs = lax.axis_size("hrs")
    panels = lax.all_to_all(fields, ("pts", "hrs"), split_axis=1, concat_axis=0, tiled=True)
    n_points = panels.shape[1] * n_pts * n_hrs
    sketched = jnp.dot(probes, panels, precision=highest, preferred_element_type=jnp.float32)
    cross_sum = lax.psum(contract_last(sketched, panels) / n_points, ("pts", "hrs"))
    local_gram = contract_last(sketched, sketched) / n_points
    gram_sum = lax.psum(local_gram, ("pts", "hrs"))
    factor = jnp.linalg.cholesky(gram_sum)
    basis_rows = lax.linalg.triangular_solve(factor, sketched, left_side=True, lower=True)
    coeffs = lax.linalg.triangular_solve(factor, cross_sum, left_side=True, lower=True)
    return (basis_rows, coeffs)


def solution(mesh):
    return jax.shard_map(
        on_device,
        mesh=mesh,
        in_specs=(P(("pts", "hrs"), None), P()),
        out_specs=(P(None, ("pts", "hrs")), P()),
        check_vma=False,
    )
```

profile of v0, /device:TPU:0, one launch (start us, length us, event | category | flops | bytes accessed | tf_op | source)
XLA Modules:
  0.0 328.4 jit_solution(12238962326394786213)
XLA Ops:
  7.2 0.0 copy-start
  7.2 0.0 all-reduce.4.cloned.1.call-start
  7.2 2.5 copy.17
  9.7 100.7 %all_to_all.19 = f32[16,32,2048]{2,0,1:T(8,128)S(1)} all-to-all(f32[16,32,2048]{2,0,1:T(8,128)S(1)} %bitcast.50), channel_id=1, replica_groups=mesh['pts'=8,'hrs'=4] {'pts','hrs'}, dimensions={1} | all-to-all | bytes 8388608 | tf_op jit(solution)/shard_map/all_to_all | solution.py:18
  110.5 0.0 copy-done
  110.5 3.7 %fusion.13 = f32[256,2048]{1,0:T(8,128)S(1)} fusion(f32[256,512]{1,0:T(8,128)S(1)} %copy-done, f32[512,2048]{1,0:T(8,128)S(1)} %bitcast.48), kind=kOutput, calls=%fused_computation.38 | convolution fusion | flops 3221225472 | bytes 6815744 | tf_op jit(solution)/shard_map/dot_general | solution.py:20
  114.2 4.5 %convolution_multiply_fusion = f32[256,512]{1,0:T(8,128)} fusion(f32[256,2048]{1,0:T(8,128)S(1)} %fusion.13, f32[512,2048]{1,0:T(8,128)S(1)} %bitcast.49), kind=kOutput, calls=%fused_computation.5 | convolution fusion | flops 3221356544 | bytes 6815744 | tf_op jit(solution)/shard_map/dot_general | solution.py:10
  118.7 2.6 convolution_multiply_fusion.1
  121.3 0.0 all-reduce.4.cloned.1.call-update
  121.3 129.5 %all-reduce.4.cloned.1.call-done = (f32[256,256]{0,1:T(8,128)}, f32[256,512]{1,0:T(8,128)}) async-done(((f32[256,256]{0,1:T(8,128)}, f32[256,512]{1,0:T(8,128)}), (f32[256,256]{0,1:T(8,128)}, f32[256,512]{1,0:T(8,128)})) %all-reduce.4.cloned.1.call-update) | async-done | bytes 786448 | tf_op jit(solution)/shard_map/psum | solution.py:23
  250.9 1.1 copy.13
  252.0 1.0 fusion.4
  253.0 11.9 %cholesky.50 = f32[128,128]{1,0:T(8,128)S(1)} custom-call(f32[128,128]{1,0:T(8,128)S(1)} %cholesky.118), custom_call_target="Cholesky" | custom-call | tf_op jit(solution)/shard_map/jit(cholesky)/cholesky | solution.py:24
  264.9 9.8 %custom-call.16 = f32[1,128,128]{1,2,0:T(8,128)S(1)} custom-call(f32[1,128,128]{2,1,0:T(8,128)S(1)} %get-tuple-element.25), custom_call_target="InvertDiagBlocksLowerTriangular" | custom-call | tf_op jit(solution)/shard_map/jit(cholesky)/cholesky | solution.py:24
  274.7 0.2 constant_dynamic-update-slice_fusion.1
  274.9 0.3 convolution_subtract_fusion.2
  275.2 11.7 %cholesky.105 = f32[128,128]{1,0:T(8,128)S(1)} custom-call(f32[128,128]{1,0:T(8,128)S(1)} %convolution_subtract_fusion.2), custom_call_target="Cholesky" | custom-call | tf_op jit(solution)/shard_map/jit(cholesky)/cholesky | solution.py:24
  287.0 0.6 compare_reduce_fusion
  288.9 0.1 triangular_solve.72
  289.0 4.0 %while.1 = (s32[]{:T(128)}, f32[256,256]{1,0:T(8,128)S(1)}, s32[2,2]{1,0:T(2,128)S(1)}, f32[2,128,128]{2,1,0:T(8,128)S(1)}, s32[]{:T(128)}) while((s32[]{:T(128)}, f32[256,256]{1,0:T(8,128)S(1)}, s32[2,2]{1,0:T(2,128)S(1)}, f32[2,128,128]{2,1,0:T(8,128)S(1)}, s32[]{:T(128)}) %tuple.27), condition=%wide.while_cond, body=%wide.while_body.sunk | while | flops 2 | bytes 131181 | solution.py:25
  289.0 0.6 fusion.27
  289.6 1.4 bitcast_dynamic-update-slice_fusion.2
  291.0 0.6 fusion.27
  291.6 1.4 bitcast_dynamic-update-slice_fusion.2
  293.0 19.9 %custom-call.17 = f32[2,128,128]{1,2,0:T(8,128)S(1)} custom-call(f32[2,128,128]{2,1,0:T(8,128)S(1)} %get-tuple-element.9), custom_call_target="InvertDiagBlocksLowerTriangular" | custom-call | tf_op jit(solution)/shard_map/triangular_solve | solution.py:25
  312.9 1.1 fusion
  314.0 1.4 fusion.2
  315.3 1.3 convolution_subtract_fusion.1
  316.7 0.4 fusion.8
  317.1 0.8 pad_maximum_fusion.1
  317.9 1.0 convolution_subtract_fusion
  319.0 1.0 fusion.9
  320.0 1.5 pad_maximum_fusion
  (9 shorter events, 0.1 us)
Async XLA Ops:
  7.2 103.3 %copy-start = (f32[256,512]{1,0:T(8,128)S(1)}, f32[256,512]{1,0:T(8,128)}, u32[]{:S(2)}) copy-start(f32[256,512]{1,0:T(8,128)} %param.3) | copy-start | bytes 1572868
  7.2 243.7 %all-reduce.4.cloned.1.call-start = ((), (), s32[]{:S(2)}) async-start(), calls=%async_computation.1 | async-start | bytes 1572864 | tf_op jit(solution)/shard_map/psum | solution.py:23
Sparse Core Ops, SparseCore 0:
  121.4 129.3 all-reduce.3
where the time goes:
time: 329 us; the launch traced here: 328 us
  waiting for transfers between devices  130 us (40%)
  blocking collectives  101 us (31%)
  other arithmetic  57.4 us (17%)
  matrix products  17.5 us (5%)
  between operations  15.5 us (5%)
  local copies, waits for them, and re-layouts  7.64 us (2%)
    psum x1, waiting for transfers between devices, on_device(): gram_sum = lax.psum(local_gram, ('pts', 'hrs'))  130 us
    all_to_all x1, blocking collectives, on_device(): lax.all_to_all(fields, ('pts', 'hrs'), split_axis=1, concat_axis=0, tiled...  101 us
    another operation x6, other arithmetic, on_device(): factor = jnp.linalg.cholesky(gram_sum)  34.1 us
    another operation x4, other arithmetic, on_device(): lax.linalg.triangular_solve(factor, sketched, left_side=True, lower=True)  21.5 us
    dot_general x2, matrix products, contract_last(): lax.dot_general(left, right, (((1,), (1,)), ((), ())), precision=highest,...  7.09 us
  transfers between devices with their start and end apart: 1, of which 1 were waited for; matrix products, arithmetic and copies ran while one was open for 0% of the time, Pallas kernels for 0%

commit v1 on v0

--- a/solution.py
+++ b/solution.py
@@ -20,7 +20,9 @@
     sketched = jnp.dot(probes, panels, precision=highest, preferred_element_type=jnp.float32)
     cross_sum = lax.psum(contract_last(sketched, panels) / n_points, ("pts", "hrs"))
     local_gram = contract_last(sketched, sketched) / n_points
-    gram_sum = lax.psum(local_gram, ("pts", "hrs"))
+    gram_sum = local_gram
+    for m in ("hrs", "pts"):
+        gram_sum = lax.psum(gram_sum, axis_name=m)
     factor = jnp.linalg.cholesky(gram_sum)
     basis_rows = lax.linalg.triangular_solve(factor, sketched, left_side=True, lower=True)
     coeffs = lax.linalg.triangular_solve(factor, cross_sum, left_side=True, lower=True)

time: 329 us -> 372 us (1.13)
  waiting for transfers between devices: 130 us -> 170 us
    psum x1 -> x3, waiting for transfers between devices: 130 us -> 170 us  [the longest x2 98.9 us: on_device(): gram_sum = lax.psum(gram_sum, axis_name=m)]
  transfers between devices with their start and end apart: 1 -> 3, of which waited for: 1 -> 3; matrix products, arithmetic and copies ran while one was open for 0% -> 19% of each run, Pallas kernels for 0% -> 0%
where the time goes in v1:
time: 372 us
  waiting for transfers between devices  170 us (46%)
  blocking collectives  101 us (27%)
  other arithmetic  57.3 us (15%)
  matrix products  20.7 us (6%)
  between operations  15.2 us (4%)
  local copies, waits for them, and re-layouts  7.74 us (2%)
    all_to_all x1, blocking collectives, on_device(): lax.all_to_all(fields, ('pts', 'hrs'), split_axis=1, concat_axis=0, tiled...  101 us
    psum x2, waiting for transfers between devices, on_device(): gram_sum = lax.psum(gram_sum, axis_name=m)  98.9 us
    psum x1, waiting for transfers between devices, on_device(): lax.psum(contract_last(sketched, panels) / n_points, ('pts', 'hrs'))  71 us
    another operation x6, other arithmetic, on_device(): factor = jnp.linalg.cholesky(gram_sum)  34.2 us
    another operation x4, other arithmetic, on_device(): lax.linalg.triangular_solve(factor, sketched, left_side=True, lower=True)  21.2 us
    dot_general x2, matrix products, contract_last(): lax.dot_general(left, right, (((1,), (1,)), ((), ())), precision=highest,...  9.23 us
  transfers between devices with their start and end apart: 3, of which 3 were waited for; matrix products, arithmetic and copies ran while one was open for 19% of the time, Pallas kernels for 0%

profile of v1, /device:TPU:0, one launch (start us, length us, event | category | flops | bytes accessed | tf_op | source)
XLA Modules:
  0.0 371.8 jit_solution(4214430342743891611)
XLA Ops:
  7.2 0.0 copy-start
  7.2 0.0 all-reduce.5.cloned.1.call-start
  7.2 2.5 copy.17
  9.7 100.7 %all_to_all.19 = f32[16,32,2048]{2,0,1:T(8,128)S(1)} all-to-all(f32[16,32,2048]{2,0,1:T(8,128)S(1)} %bitcast.50), channel_id=1, replica_groups=mesh['pts'=8,'hrs'=4] {'pts','hrs'}, dimensions={1} | all-to-all | bytes 8388608 | tf_op jit(solution)/shard_map/all_to_all | solution.py:18
  110.5 0.0 copy-start.1
  110.5 0.0 copy-done
  110.5 3.7 fusion.13
  114.2 0.0 copy-done.1
  114.2 2.6 convolution_multiply_fusion.1
  116.8 0.0 all-reduce.5.cloned.1.call-update
  116.8 0.0 all-reduce.7.cloned.1.call-start
  116.9 31.4 %all-reduce.5.cloned.1.call-done = f32[256,256]{0,1:T(8,128)} async-done(((f32[256,256]{0,1:T(8,128)}), f32[256,256]{0,1:T(8,128)}) %all-reduce.5.cloned.1.call-update) | async-done | bytes 262160 | tf_op jit(solution)/shard_map/psum | solution.py:25
  148.3 0.0 all-reduce.7.cloned.1.call-update
  148.3 0.2 all-reduce.9.cloned.1.call-start
  148.5 6.7 %convolution_multiply_fusion = f32[256,512]{1,0:T(8,128)} fusion(f32[256,2048]{1,0:T(8,128)S(1)} %fusion.13, f32[512,2048]{1,0:T(8,128)} %bitcast.49), kind=kOutput, calls=%fused_computation.5 | convolution fusion | flops 3221356544 | bytes 6815744 | tf_op jit(solution)/shard_map/dot_general | solution.py:10
  155.2 0.0 all-reduce.9.cloned.1.call-update
  155.2 67.5 %all-reduce.7.cloned.1.call-done = f32[256,256]{0,1:T(8,128)} async-done(((f32[256,256]{0,1:T(8,128)}), f32[256,256]{0,1:T(8,128)}) %all-reduce.7.cloned.1.call-update) | async-done | bytes 262160 | tf_op jit(solution)/shard_map/psum | solution.py:25
  222.7 1.1 copy.13
  223.8 1.0 fusion.4
  224.8 11.7 %cholesky.50 = f32[128,128]{1,0:T(8,128)S(1)} custom-call(f32[128,128]{1,0:T(8,128)S(1)} %cholesky.118), custom_call_target="Cholesky" | custom-call | tf_op jit(solution)/shard_map/jit(cholesky)/cholesky | solution.py:26
  236.5 9.8 %custom-call.16 = f32[1,128,128]{1,2,0:T(8,128)S(1)} custom-call(f32[1,128,128]{2,1,0:T(8,128)S(1)} %get-tuple-element.23), custom_call_target="InvertDiagBlocksLowerTriangular" | custom-call | tf_op jit(solution)/shard_map/jit(cholesky)/cholesky | solution.py:26
  246.4 0.2 constant_dynamic-update-slice_fusion.1
  246.6 0.3 convolution_subtract_fusion.2
  246.9 11.9 %cholesky.105 = f32[128,128]{1,0:T(8,128)S(1)} custom-call(f32[128,128]{1,0:T(8,128)S(1)} %convolution_subtract_fusion.2), custom_call_target="Cholesky" | custom-call | tf_op jit(solution)/shard_map/jit(cholesky)/cholesky | solution.py:26
  258.8 0.7 compare_reduce_fusion
  260.8 0.1 triangular_solve.72
  260.9 4.1 %while.1 = (s32[]{:T(128)}, f32[256,256]{1,0:T(8,128)S(1)}, s32[2,2]{1,0:T(2,128)S(1)}, f32[2,128,128]{2,1,0:T(8,128)S(1)}, s32[]{:T(128)}) while((s32[]{:T(128)}, f32[256,256]{1,0:T(8,128)S(1)}, s32[2,2]{1,0:T(2,128)S(1)}, f32[2,128,128]{2,1,0:T(8,128)S(1)}, s32[]{:T(128)}) %tuple.27), condition=%wide.while_cond, body=%wide.while_body.sunk | while | flops 2 | bytes 131181 | solution.py:27
  260.9 0.7 fusion.27
  261.6 1.3 bitcast_dynamic-update-slice_fusion.2
  262.9 0.7 fusion.27
  263.6 1.3 bitcast_dynamic-update-slice_fusion.2
  265.0 19.7 %custom-call.17 = f32[2,128,128]{1,2,0:T(8,128)S(1)} custom-call(f32[2,128,128]{2,1,0:T(8,128)S(1)} %get-tuple-element.9), custom_call_target="InvertDiagBlocksLowerTriangular" | custom-call | tf_op jit(solution)/shard_map/triangular_solve | solution.py:27
  284.7 2.0 fusion
  286.7 71.0 %all-reduce.9.cloned.1.call-done = f32[256,512]{1,0:T(8,128)} async-done(((f32[256,512]{1,0:T(8,128)}), f32[256,512]{1,0:T(8,128)}) %all-reduce.9.cloned.1.call-update) | async-done | bytes 524304 | tf_op jit(solution)/shard_map/psum | solution.py:21
  357.6 0.0 copy-start.2
  357.6 1.5 fusion.2
  359.1 1.3 convolution_subtract_fusion.1
  360.4 0.4 fusion.8
  360.9 0.8 pad_maximum_fusion.1
  361.7 0.0 copy-done.2
  361.7 1.0 convolution_subtract_fusion
  362.7 1.1 fusion.9
  363.8 1.5 pad_maximum_fusion
  (9 shorter events, 0.1 us)
Async XLA Ops:
  7.2 103.3 %copy-start = (f32[256,512]{1,0:T(8,128)S(1)}, f32[256,512]{1,0:T(8,128)}, u32[]{:S(2)}) copy-start(f32[256,512]{1,0:T(8,128)} %param.3) | copy-start | bytes 1572868
  7.2 141.1 %all-reduce.5.cloned.1.call-start = ((), (), s32[]{:S(2)}) async-start(), calls=%async_computation.1 | async-start | bytes 524288 | tf_op jit(solution)/shard_map/psum | solution.py:25
  110.5 3.7 copy-start.1
  116.8 105.9 %all-reduce.7.cloned.1.call-start = ((), (), s32[]{:S(2)}) async-start(), calls=%async_computation.2 | async-start | bytes 524288 | tf_op jit(solution)/shard_map/psum | solution.py:25
  148.3 209.3 %all-reduce.9.cloned.1.call-start = ((), (), s32[]{:S(2)}) async-start(), calls=%async_computation.3 | async-start | bytes 1048576 | tf_op jit(solution)/shard_map/psum | solution.py:21
  357.6 4.1 %copy-start.2 = (f32[128,2048]{1,0:T(8,128)S(1)}, f32[128,2048]{1,0:T(8,128)}, u32[]{:S(2)}) copy-start(f32[128,2048]{1,0:T(8,128)} %fusion) | copy-start | bytes 3145732
Sparse Core Ops, SparseCore 0:
  116.9 31.3 all-reduce.4
  151.6 71.0 all-reduce.6
  228.6 129.0 all-reduce.8
